TPU v7x, 32 devices: a whole 2x2x4 slice. The times are simulated.
32 devices in a mesh: prow: 2 (over x), pcol: 16 (over z, y, core).
Axes of the slice: x: 2, y: 2, z: 4, core: 2. Of those that a mesh axis runs over, the one named last changes fastest.
Arguments:
- vectors: float32 [32768, 2048], P('prow', 'pcol'), may hold values from -6 to 6
- reflectors: bfloat16 [4, 256, 32768], P(None, 'pcol', 'prow'), may hold values from -0.03125 to 0.03125
- tau_diag: float32 [4, 256], replicated, may hold values from 0.5 to 1.5
- coupling: float32 [4, 256, 256], replicated, may hold values from -0.375 to 0.375
Outputs:
- result: float32 [32768, 2048], P('prow', 'pcol')
All inputs are finite; a program needn't handle non-finite values.
Results may differ from a plain program's by a relative error of at most 0.0003.
Values may be sent and summed in bfloat16 or wider, within the bound.
A program may use at most 128 MiB of HBM per device.

v0:
```python
import jax
import jax.numpy as jnp
from jax import lax
from jax.sharding import PartitionSpec as P


def on_device(vectors, reflectors, tau_diag, coupling):
    count = reflectors.shape[0]
    gathered = lax.all_gather(reflectors, "pcol", axis=1, tiled=True)
    current = vectors
    for position in range(count - 1, -1, -1):
        rows_panel = gathered[position]
        widened = rows_panel.astype(jnp.float32)
        tri_factor = jnp.diag(tau_diag[position]) + jnp.triu(coupling[position], 1)
        partial_sum = jnp.dot(
            widened, current, precision=lax.Precision.HIGHEST, preferred_element_type=jnp.float32
        )
        totals = lax.psum(partial_sum, "prow")
        updates = jnp.dot(
            tri_factor, totals, precision=lax.Precision.HIGHEST, preferred_element_type=jnp.float32
        )
        current = current - lax.dot_general(
            widened,
            updates,
            (((0,), (0,)), ((), ())),
            precision=lax.Precision.HIGHEST,
            preferred_element_type=jnp.float32,
        )
    return current


def solution(mesh):
    return jax.shard_map(
        on_device,
        mesh=mesh,
        in_specs=(P("prow", "pcol"), P(None, "pcol", "prow"), P(), P()),
        out_specs=P("prow", "pcol"),
        check_vma=False,
    )
```

profile of v0, /device:TPU:0, one launch (start us, length us, event | category | flops | bytes accessed | tf_op | source)
XLA Modules:
  0.0 387.4 jit_solution(3231491931866824591)
XLA Ops:
  6.5 0.0 all-gather.2.cloned.1.call-start
  6.5 0.7 all-gather.2.cloned.1.call-update
  7.3 0.0 all-reduce.5.cloned.1.call-start
  7.3 9.0 %copy.5 = f32[16384,128]{0,1:T(8,128)} copy(f32[16384,128]{1,0:T(8,128)} %param.4) | data formatting | bytes 16777216 | tf_op args[0]
  16.3 0.0 copy-start.3
  16.3 0.0 copy-start.4
  16.3 163.4 %all-gather.2.cloned.1.call-done = bf16[4,256,16384]{2,1,0:T(8,128)(2,1)} async-done(((bf16[4,16,16384]{2,1,0:T(8,128)(2,1)}), bf16[4,256,16384]{2,1,0:T(8,128)(2,1)}) %all-gather.2.cloned.1.call-update) | async-done | bytes 33554448 | tf_op jit(solution)/shard_map/all_gather | solution.py:9
  179.7 11.2 %fusion.4 = f32[256,128]{1,0:T(8,128)} fusion(f32[16384,128]{1,0:T(8,128)} %param.4, bf16[4,256,16384]{2,1,0:T(8,128)(2,1)} %all-gather.2.cloned.1.call-done), kind=kOutput, calls=%fused_computation.12 | convolution fusion | flops 6442450944 | bytes 16908288 | tf_op jit(solution)/shard_map/dot_general | solution.py:15
  190.9 0.0 all-reduce.5.cloned.1.call-update
  190.9 0.6 all-reduce.7.cloned.1.call-start
  191.5 0.0 copy-done.3
  191.5 21.1 %all-reduce.5.cloned.1.call-done = f32[256,128]{1,0:T(8,128)} async-done(((f32[256,128]{1,0:T(8,128)}), f32[256,128]{1,0:T(8,128)}) %all-reduce.5.cloned.1.call-update) | async-done | bytes 131088 | tf_op jit(solution)/shard_map/psum | solution.py:18
  212.6 0.0 copy-done.4
  212.6 1.3 fusion.21
  213.9 9.4 %fusion.3 = f32[16384,128]{0,1:T(8,128)S(1)} fusion(f32[16384,128]{0,1:T(8,128)} %copy.5, f32[256,128]{1,0:T(8,128)S(1)} %fusion.21, bf16[4,256,16384]{2,1,0:T(8,128)(2,1)} %all-gather.2.cloned.1.call-done), kind=kOutput, calls=%fused_computation.7 | convolution fusion | flops 6444548096 | bytes 25296896 | tf_op jit(solution)/shard_map/dot_general | solution.py:22
  223.3 0.0 copy-start
  223.3 3.4 copy-done
  226.7 12.5 %fusion.10 = f32[256,128]{0,1:T(8,128)} fusion(f32[16384,128]{0,1:T(8,128)S(1)} %fusion.3, bf16[4,256,16384]{2,1,0:T(8,128)(2,1)} %all-gather.2.cloned.1.call-done), kind=kOutput, calls=%fused_computation.18 | convolution fusion | flops 6442450944 | bytes 16908288 | tf_op jit(solution)/shard_map/dot_general | solution.py:15
  239.2 0.0 all-reduce.7.cloned.1.call-update
  239.2 0.2 all-reduce.9.cloned.1.call-start
  239.4 21.5 %all-reduce.7.cloned.1.call-done = f32[256,128]{0,1:T(8,128)} async-done(((f32[256,128]{0,1:T(8,128)}), f32[256,128]{0,1:T(8,128)}) %all-reduce.7.cloned.1.call-update) | async-done | bytes 131088 | tf_op jit(solution)/shard_map/psum | solution.py:18
  260.9 1.3 fusion.18
  262.2 9.4 %fusion.2 = f32[16384,128]{0,1:T(8,128)S(1)} fusion(f32[16384,128]{0,1:T(8,128)} %copy-done, f32[256,128]{1,0:T(8,128)S(1)} %fusion.18, bf16[4,256,16384]{2,1,0:T(8,128)(2,1)} %all-gather.2.cloned.1.call-done), kind=kOutput, calls=%fused_computation.5 | convolution fusion | flops 6444548096 | bytes 25296896 | tf_op jit(solution)/shard_map/dot_general | solution.py:22
  271.6 0.0 copy-start.1
  271.6 3.4 copy-done.1
  275.0 12.5 %fusion.9 = f32[256,128]{0,1:T(8,128)} fusion(f32[16384,128]{0,1:T(8,128)S(1)} %fusion.2, bf16[4,256,16384]{2,1,0:T(8,128)(2,1)} %all-gather.2.cloned.1.call-done), kind=kOutput, calls=%fused_computation.17 | convolution fusion | flops 6442450944 | bytes 16908288 | tf_op jit(solution)/shard_map/dot_general | solution.py:15
  287.5 0.0 all-reduce.9.cloned.1.call-update
  287.5 0.3 all-reduce.11.cloned.1.call-start
  287.8 21.4 %all-reduce.9.cloned.1.call-done = f32[256,128]{0,1:T(8,128)} async-done(((f32[256,128]{0,1:T(8,128)}), f32[256,128]{0,1:T(8,128)}) %all-reduce.9.cloned.1.call-update) | async-done | bytes 131088 | tf_op jit(solution)/shard_map/psum | solution.py:18
  309.2 1.3 fusion.15
  310.5 9.4 %fusion.1 = f32[16384,128]{0,1:T(8,128)S(1)} fusion(f32[16384,128]{0,1:T(8,128)} %copy-done.1, f32[256,128]{1,0:T(8,128)S(1)} %fusion.15, bf16[4,256,16384]{2,1,0:T(8,128)(2,1)} %all-gather.2.cloned.1.call-done), kind=kOutput, calls=%fused_computation.3 | convolution fusion | flops 6444548096 | bytes 25296896 | tf_op jit(solution)/shard_map/dot_general | solution.py:22
  319.9 0.0 copy-start.2
  319.9 3.4 copy-done.2
  323.3 12.5 %fusion.8 = f32[256,128]{0,1:T(8,128)} fusion(f32[16384,128]{0,1:T(8,128)S(1)} %fusion.1, bf16[4,256,16384]{2,1,0:T(8,128)(2,1)} %all-gather.2.cloned.1.call-done), kind=kOutput, calls=%fused_computation.16 | convolution fusion | flops 6442450944 | bytes 16908288 | tf_op jit(solution)/shard_map/dot_general | solution.py:15
  335.7 0.0 all-reduce.11.cloned.1.call-update
  335.8 21.7 %all-reduce.11.cloned.1.call-done = f32[256,128]{0,1:T(8,128)} async-done(((f32[256,128]{0,1:T(8,128)}), f32[256,128]{0,1:T(8,128)}) %all-reduce.11.cloned.1.call-update) | async-done | bytes 131088 | tf_op jit(solution)/shard_map/psum | solution.py:18
  357.5 1.3 fusion.12
  358.8 12.8 %fusion = f32[16384,128]{0,1:T(8,128)} fusion(f32[16384,128]{0,1:T(8,128)} %copy-done.2, f32[256,128]{1,0:T(8,128)S(1)} %fusion.12, bf16[4,256,16384]{2,1,0:T(8,128)(2,1)} %all-gather.2.cloned.1.call-done), kind=kOutput, calls=%fused_computation.1 | convolution fusion | flops 6444548096 | bytes 25296896 | tf_op jit(solution)/shard_map/dot_general | solution.py:22
  371.6 9.0 %copy.6 = f32[16384,128]{1,0:T(8,128)} copy(f32[16384,128]{0,1:T(8,128)} %fusion) | data formatting | bytes 16777216 | tf_op jit(solution)/shard_map/sub | solution.py:22
  (1 shorter events, 0.0 us)
Async XLA Ops:
  6.5 173.1 %all-gather.2.cloned.1.call-start = ((), (), s32[]{:S(2)}) async-start(), calls=%async_computation | async-start | bytes 35651584 | tf_op jit(solution)/shard_map/all_gather | solution.py:9
  7.3 205.4 %all-reduce.5.cloned.1.call-start = ((), (), s32[]{:S(2)}) async-start(), calls=%async_computation.1 | async-start | bytes 262144 | tf_op jit(solution)/shard_map/psum | solution.py:18
  16.3 175.2 %copy-start.3 = (f32[4,256]{1,0:T(4,128)S(1)}, f32[4,256]{1,0:T(4,128)}, u32[]{:S(2)}) copy-start(f32[4,256]{1,0:T(4,128)} %param.6) | copy-start | bytes 12292
  16.3 196.3 %copy-start.4 = (f32[4,256,256]{2,1,0:T(8,128)S(1)}, f32[4,256,256]{2,1,0:T(8,128)}, u32[]{:S(2)}) copy-start(f32[4,256,256]{2,1,0:T(8,128)} %param.7) | copy-start | bytes 3145732
  190.9 70.0 %all-reduce.7.cloned.1.call-start = ((), (), s32[]{:S(2)}) async-start(), calls=%async_computation.2 | async-start | bytes 262144 | tf_op jit(solution)/shard_map/psum | solution.py:18
  223.3 3.4 copy-start
  239.2 70.0 %all-reduce.9.cloned.1.call-start = ((), (), s32[]{:S(2)}) async-start(), calls=%async_computation.3 | async-start | bytes 262144 | tf_op jit(solution)/shard_map/psum | solution.py:18
  271.6 3.4 copy-start.1
  287.5 70.0 %all-reduce.11.cloned.1.call-start = ((), (), s32[]{:S(2)}) async-start(), calls=%async_computation.4 | async-start | bytes 262144 | tf_op jit(solution)/shard_map/psum | solution.py:18
  319.9 3.4 copy-start.2
Sparse Core Ops, SparseCore 0:
  8.9 170.7 all-gather.1
  191.1 21.5 all-reduce.4
  239.3 21.5 all-reduce.6
  287.6 21.5 all-reduce.8
  335.9 21.5 all-reduce.10
where the time goes:
time: 391 us; the launch traced here: 387 us
  waiting for transfers between devices  250 us (64%)
  matrix products  94.8 us (24%)
  local copies, waits for them, and re-layouts  28.2 us (7%)
  between operations  13.5 us (3%)
    all_gather x1, waiting for transfers between devices, on_device(): gathered = lax.all_gather(reflectors, 'pcol', axis=1, tiled=True)  163 us
    psum x4, waiting for transfers between devices, on_device(): totals = lax.psum(partial_sum, 'prow')  85.7 us
    dot_general x4, matrix products, on_device(): jnp.dot(widened, current, precision=lax.Precision.HIGHEST, preferred_elem...  48.7 us
    dot_general x4, matrix products, on_device(): lax.dot_general(widened, updates, (((0,), (0,)), ((), ())), precision=lax...  40.9 us
    unnamed x11, local copies, waits for them, and re-layouts  19.2 us
    sub x1, local copies, waits for them, and re-layouts, on_device(): current - lax.dot_general(widened, updates, (((0,), (0,)), ((), ())), pre...  8.98 us
  transfers between devices with their start and end apart: 5, of which 5 were waited for; matrix products, arithmetic and copies ran while one was open for 2% of the time, Pallas kernels for 0%

commit v1 on v0

--- a/solution.py
+++ b/solution.py
@@ -15,7 +15,7 @@
         partial_sum = jnp.dot(
             widened, current, precision=lax.Precision.HIGHEST, preferred_element_type=jnp.float32
         )
-        totals = lax.psum(partial_sum, "prow")
+        totals = jnp.sum(lax.all_gather(partial_sum, "prow"), axis=0)
         updates = jnp.dot(
             tri_factor, totals, precision=lax.Precision.HIGHEST, preferred_element_type=jnp.float32
         )

time: 391 us -> 324 us (0.83)
  waiting for transfers between devices: 250 us -> 164 us
  blocking collectives: 0 us -> 24.4 us
  local copies, waits for them, and re-layouts: 28.2 us -> 18.5 us
    psum x4 -> x0, waiting for transfers between devices: 85.7 us -> none  [on_device(): totals = lax.psum(partial_sum, 'prow')]
    all_gather x0 -> x4, blocking collectives: none -> 24.4 us  [on_device(): totals = jnp.sum(lax.all_gather(partial_sum, 'prow'), axis=0)]
    unnamed x11, local copies, waits for them, and re-layouts: 19.2 us -> 9.03 us
    dot_general x4, matrix products: 48.7 us -> 55.2 us  [on_device(): jnp.dot(widened, current, precision=lax.Precision.HIGHEST, preferred_elem...]
  transfers between devices with their start and end apart: 5 -> 1, of which waited for: 5 -> 1; matrix products, arithmetic and copies ran while one was open for 2% -> 3% of each run, Pallas kernels for 0% -> 0%
where the time goes in v1:
time: 324 us; the launch traced here: 319 us
  waiting for transfers between devices  164 us (51%)
  matrix products  97.5 us (30%)
  blocking collectives  24.4 us (8%)
  local copies, waits for them, and re-layouts  18.5 us (6%)
  between operations  13.8 us (4%)
    all_gather x1, waiting for transfers between devices, on_device(): gathered = lax.all_gather(reflectors, 'pcol', axis=1, tiled=True)  163 us
    dot_general x4, matrix products, on_device(): jnp.dot(widened, current, precision=lax.Precision.HIGHEST, preferred_elem...  55.2 us
    dot_general x4, matrix products, on_device(): lax.dot_general(widened, updates, (((0,), (0,)), ((), ())), precision=lax...  40.6 us
    all_gather x4, blocking collectives, on_device(): totals = jnp.sum(lax.all_gather(partial_sum, 'prow'), axis=0)  24.4 us
    unnamed x11, local copies, waits for them, and re-layouts  9.03 us
    sub x1, local copies, waits for them, and re-layouts, on_device(): current - lax.dot_general(widened, updates, (((0,), (0,)), ((), ())), pre...  8.98 us
  transfers between devices with their start and end apart: 1, of which 1 were waited for; matrix products, arithmetic and copies ran while one was open for 3% of the time, Pallas kernels for 0%

profile of v1, /device:TPU:0, one launch (start us, length us, event | category | flops | bytes accessed | tf_op | source)
XLA Modules:
  0.0 319.3 jit_solution(994207553898022078)
XLA Ops:
  6.5 0.0 all-gather.6.cloned.1.call-start
  6.5 0.7 all-gather.6.cloned.1.call-update
  7.3 0.0 copy-start.3
  7.3 9.0 %copy.7 = f32[16384,128]{0,1:T(8,128)} copy(f32[16384,128]{1,0:T(8,128)} %param.4) | data formatting | bytes 16777216 | tf_op args[0]
  16.3 0.0 copy-done.3
  16.3 0.0 copy-start.4
  16.3 163.4 %all-gather.6.cloned.1.call-done = bf16[4,256,16384]{2,1,0:T(8,128)(2,1)} async-done(((bf16[4,16,16384]{2,1,0:T(8,128)(2,1)}), bf16[4,256,16384]{2,1,0:T(8,128)(2,1)}) %all-gather.6.cloned.1.call-update) | async-done | bytes 33554448 | tf_op jit(solution)/shard_map/all_gather | solution.py:9
  179.7 10.6 %fusion.4 = f32[256,128]{1,0:T(8,128)S(1)} fusion(f32[16384,128]{1,0:T(8,128)} %param.4, bf16[4,256,16384]{2,1,0:T(8,128)(2,1)} %all-gather.6.cloned.1.call-done), kind=kOutput, calls=%fused_computation.12 | convolution fusion | flops 6442450944 | bytes 16908288 | tf_op jit(solution)/shard_map/dot_general | solution.py:15
  190.3 6.6 %all-gather = f32[512,128]{1,0:T(8,128)S(1)} all-gather(f32[256,128]{1,0:T(8,128)S(1)} %fusion.4), channel_id=2, replica_groups=mesh['prow'=2,'pcol'=16] {'prow'}, dimensions={0}, use_global_device_ids=true | all-gather | bytes 393216 | tf_op jit(solution)/shard_map/all_gather | solution.py:18
  196.9 0.0 copy-done.4
  196.9 0.4 fusion.21
  197.4 9.4 %fusion.3 = f32[16384,128]{0,1:T(8,128)S(1)} fusion(f32[16384,128]{0,1:T(8,128)} %copy.7, f32[256,128]{1,0:T(8,128)S(1)} %fusion.21, bf16[4,256,16384]{2,1,0:T(8,128)(2,1)} %all-gather.6.cloned.1.call-done), kind=kOutput, calls=%fused_computation.7 | convolution fusion | flops 6444548096 | bytes 25296896 | tf_op jit(solution)/shard_map/dot_general | solution.py:22
  206.7 0.0 copy-start.1
  206.7 14.9 %fusion.10 = f32[256,128]{0,1:T(8,128)S(1)} fusion(f32[16384,128]{0,1:T(8,128)S(1)} %fusion.3, bf16[4,256,16384]{2,1,0:T(8,128)(2,1)} %all-gather.6.cloned.1.call-done), kind=kOutput, calls=%fused_computation.18 | convolution fusion | flops 6442450944 | bytes 16908288 | tf_op jit(solution)/shard_map/dot_general | solution.py:15
  221.6 0.0 copy-done.1
  221.6 6.2 %all-gather.1 = f32[512,128]{0,1:T(8,128)S(1)} all-gather(f32[256,128]{0,1:T(8,128)S(1)} %fusion.10), channel_id=3, replica_groups=mesh['prow'=2,'pcol'=16] {'prow'}, dimensions={0}, use_global_device_ids=true | all-gather | bytes 393216 | tf_op jit(solution)/shard_map/all_gather | solution.py:18
  227.8 0.2 reshape.9
  228.0 0.3 reduce_sum.37
  228.3 0.4 fusion.18
  228.7 9.4 %fusion.2 = f32[16384,128]{0,1:T(8,128)S(1)} fusion(f32[16384,128]{0,1:T(8,128)} %copy-done.1, f32[256,128]{1,0:T(8,128)S(1)} %fusion.18, bf16[4,256,16384]{2,1,0:T(8,128)(2,1)} %all-gather.6.cloned.1.call-done), kind=kOutput, calls=%fused_computation.5 | convolution fusion | flops 6444548096 | bytes 25296896 | tf_op jit(solution)/shard_map/dot_general | solution.py:22
  238.1 0.0 copy-start.2
  238.1 14.9 %fusion.9 = f32[256,128]{0,1:T(8,128)S(1)} fusion(f32[16384,128]{0,1:T(8,128)S(1)} %fusion.2, bf16[4,256,16384]{2,1,0:T(8,128)(2,1)} %all-gather.6.cloned.1.call-done), kind=kOutput, calls=%fused_computation.17 | convolution fusion | flops 6442450944 | bytes 16908288 | tf_op jit(solution)/shard_map/dot_general | solution.py:15
  253.0 0.0 copy-done.2
  253.0 5.8 %all-gather.2 = f32[512,128]{0,1:T(8,128)S(1)} all-gather(f32[256,128]{0,1:T(8,128)S(1)} %fusion.9), channel_id=4, replica_groups=mesh['prow'=2,'pcol'=16] {'prow'}, dimensions={0}, use_global_device_ids=true | all-gather | bytes 393216 | tf_op jit(solution)/shard_map/all_gather | solution.py:18
  258.8 0.2 reshape.10
  259.0 0.3 reduce_sum.38
  259.3 0.4 fusion.15
  259.7 9.4 %fusion.1 = f32[16384,128]{0,1:T(8,128)S(1)} fusion(f32[16384,128]{0,1:T(8,128)} %copy-done.2, f32[256,128]{1,0:T(8,128)S(1)} %fusion.15, bf16[4,256,16384]{2,1,0:T(8,128)(2,1)} %all-gather.6.cloned.1.call-done), kind=kOutput, calls=%fused_computation.3 | convolution fusion | flops 6444548096 | bytes 25296896 | tf_op jit(solution)/shard_map/dot_general | solution.py:22
  269.1 0.0 copy-start
  269.1 14.9 %fusion.8 = f32[256,128]{0,1:T(8,128)S(1)} fusion(f32[16384,128]{0,1:T(8,128)S(1)} %fusion.1, bf16[4,256,16384]{2,1,0:T(8,128)(2,1)} %all-gather.6.cloned.1.call-done), kind=kOutput, calls=%fused_computation.16 | convolution fusion | flops 6442450944 | bytes 16908288 | tf_op jit(solution)/shard_map/dot_general | solution.py:15
  284.0 0.0 copy-done
  284.0 5.8 %all-gather.3 = f32[512,128]{0,1:T(8,128)S(1)} all-gather(f32[256,128]{0,1:T(8,128)S(1)} %fusion.8), channel_id=5, replica_groups=mesh['prow'=2,'pcol'=16] {'prow'}, dimensions={0}, use_global_device_ids=true | all-gather | bytes 393216 | tf_op jit(solution)/shard_map/all_gather | solution.py:18
  289.8 0.2 reshape.11
  290.0 0.3 reduce_sum.39
  290.3 0.4 fusion.12
  290.7 12.6 %fusion = f32[16384,128]{0,1:T(8,128)} fusion(f32[16384,128]{0,1:T(8,128)} %copy-done, f32[256,128]{1,0:T(8,128)S(1)} %fusion.12, bf16[4,256,16384]{2,1,0:T(8,128)(2,1)} %all-gather.6.cloned.1.call-done), kind=kOutput, calls=%fused_computation.1 | convolution fusion | flops 6444548096 | bytes 25296896 | tf_op jit(solution)/shard_map/dot_general | solution.py:22
  303.3 9.0 %copy.8 = f32[16384,128]{1,0:T(8,128)} copy(f32[16384,128]{0,1:T(8,128)} %fusion) | data formatting | bytes 16777216 | tf_op jit(solution)/shard_map/sub | solution.py:22
  (2 shorter events, 0.0 us)
Async XLA Ops:
  6.5 173.1 %all-gather.6.cloned.1.call-start = ((), (), s32[]{:S(2)}) async-start(), calls=%async_computation | async-start | bytes 35651584 | tf_op jit(solution)/shard_map/all_gather | solution.py:9
  7.3 9.0 %copy-start.3 = (f32[4,256]{1,0:T(4,128)S(1)}, f32[4,256]{1,0:T(4,128)}, u32[]{:S(2)}) copy-start(f32[4,256]{1,0:T(4,128)} %param.6) | copy-start | bytes 12292
  16.3 180.7 %copy-start.4 = (f32[4,256,256]{2,1,0:T(8,128)S(1)}, f32[4,256,256]{2,1,0:T(8,128)}, u32[]{:S(2)}) copy-start(f32[4,256,256]{2,1,0:T(8,128)} %param.7) | copy-start | bytes 3145732
  206.7 14.9 %copy-start.1 = (f32[16384,128]{0,1:T(8,128)}, f32[16384,128]{0,1:T(8,128)S(1)}, u32[]{:S(2)}) copy-start(f32[16384,128]{0,1:T(8,128)S(1)} %fusion.3) | copy-start | bytes 25165828
  238.1 14.9 %copy-start.2 = (f32[16384,128]{0,1:T(8,128)}, f32[16384,128]{0,1:T(8,128)S(1)}, u32[]{:S(2)}) copy-start(f32[16384,128]{0,1:T(8,128)S(1)} %fusion.2) | copy-start | bytes 25165828
  269.1 14.9 %copy-start = (f32[16384,128]{0,1:T(8,128)}, f32[16384,128]{0,1:T(8,128)S(1)}, u32[]{:S(2)}) copy-start(f32[16384,128]{0,1:T(8,128)S(1)} %fusion.1) | copy-start | bytes 25165828
Sparse Core Ops, SparseCore 0:
  8.9 170.7 all-gather.5
